TPU v7x, 32 devices: a whole 2x2x4 slice. The times are simulated.
32 devices in a mesh: batch: 4 (over z), grid: 8 (over y, x, core).
Axes of the slice: x: 2, y: 2, z: 4, core: 2. Of those that a mesh axis runs over, the one named last changes fastest.
Arguments:
- fields: bfloat16 [1024, 512, 512], P(('batch', 'grid')), parts along dimension 0, may hold values from -18 to 18
- norm_gain: float32 [256], replicated, may hold values from 0.5 to 1.5
- norm_shift: float32 [256], replicated, may hold values from -3 to 3
- first_weight: bfloat16 [2, 8, 32, 32], replicated, may hold values from -0.75 to 0.75
- second_weight: bfloat16 [2, 8, 32, 32], replicated, may hold values from -0.75 to 0.75
- first_bias: float32 [2, 256], replicated, may hold values from -2 to 2
Outputs:
- mixed_fields: bfloat16 [1024, 512, 512], P(('batch', 'grid')), parts along dimension 0
There are 4 independent parts, one for each index of `batch`. A program takes and returns all parts, laid end to end along the dimension named above; an argument that names none is the same for every part. Nothing has to cross between parts.
All inputs are finite; a program needn't handle non-finite values.
Results may differ from a plain program's by a relative error of at most 0.0055.
Values may be sent and summed in bfloat16 or wider, within the bound.
No kernel may reach another device: no remote copies, remote signals or barrier semaphores. Data moves between devices by JAX's collectives and lax.ppermute only.
A program may use at most 192 MiB of HBM per device.

v0:
```python
import math

import jax
import jax.numpy as jnp
from jax import lax
from jax.sharding import PartitionSpec as P


def tables(rows, cols):
    half = cols // 2
    col_index = jnp.arange(cols, dtype=jnp.int32)
    mode_index = jnp.arange(half, dtype=jnp.int32)
    angle_w = (col_index[:, None] * mode_index[None, :] % cols).astype(jnp.float32) * (
        2.0 * math.pi / cols
    )
    scale_w = 1.0 / math.sqrt(cols)
    fwd_w = jnp.concatenate(
        [jnp.cos(angle_w) * scale_w, -jnp.sin(angle_w) * scale_w], axis=1
    ).astype(jnp.bfloat16)
    weight_k = jnp.where(mode_index == 0, 1.0, 2.0).astype(jnp.float32)
    inv_w = jnp.concatenate(
        [
            (jnp.cos(angle_w) * weight_k[None, :] * scale_w).T,
            (-jnp.sin(angle_w) * weight_k[None, :] * scale_w).T,
        ],
        axis=0,
    ).astype(jnp.bfloat16)
    row_index = jnp.arange(rows, dtype=jnp.int32)
    angle_h = (row_index[:, None] * row_index[None, :] % rows).astype(jnp.float32) * (
        2.0 * math.pi / rows
    )
    scale_h = 1.0 / math.sqrt(rows)
    cos_h = (jnp.cos(angle_h) * scale_h).astype(jnp.bfloat16)
    sin_h = (jnp.sin(angle_h) * scale_h).astype(jnp.bfloat16)
    return (fwd_w, inv_w, cos_h, sin_h)


def mult(form, left, right):
    return jnp.einsum(form, left, right, preferred_element_type=jnp.float32)


def shrink(values):
    return jnp.maximum(values - 0.01, 0.0) + jnp.minimum(values + 0.01, 0.0)


def mix_modes(real_part, imag_part, first_weight, second_weight, first_bias):
    blocks = first_weight.shape[1]
    width = first_weight.shape[2]
    shape = real_part.shape
    real_blk = real_part.reshape(blocks, width, -1)
    imag_blk = imag_part.reshape(blocks, width, -1)
    bias_blk = first_bias.reshape(2, blocks, width, 1)
    hid_re = jax.nn.relu(
        mult("bio,bim->bom", first_weight[0], real_blk)
        - mult("bio,bim->bom", first_weight[1], imag_blk)
        + bias_blk[0]
    ).astype(jnp.bfloat16)
    hid_im = jax.nn.relu(
        mult("bio,bim->bom", first_weight[0], imag_blk)
        + mult("bio,bim->bom", first_weight[1], real_blk)
        + bias_blk[1]
    ).astype(jnp.bfloat16)
    out_re = mult("bio,bim->bom", second_weight[0], hid_re) - mult(
        "bio,bim->bom", second_weight[1], hid_im
    )
    out_im = mult("bio,bim->bom", second_weight[0], hid_im) + mult(
        "bio,bim->bom", second_weight[1], hid_re
    )
    return (
        shrink(out_re).astype(jnp.bfloat16).reshape(shape),
        shrink(out_im).astype(jnp.bfloat16).reshape(shape),
    )


def per_device(fields, norm_gain, norm_shift, first_weight, second_weight, first_bias):
    local_ch, rows, cols = fields.shape
    half = cols // 2
    groups = lax.axis_size("grid")
    channels = local_ch * groups
    fwd_w, inv_w, cos_h, sin_h = tables(rows, cols)
    values = fields.astype(jnp.float32)
    start = lax.axis_index("grid") * local_ch
    gain_own = lax.dynamic_slice_in_dim(norm_gain, start, local_ch)
    shift_own = lax.dynamic_slice_in_dim(norm_shift, start, local_ch)
    total_sum, total_sq = lax.psum(
        (jnp.sum(values, axis=0), jnp.sum(values * values, axis=0)), "grid"
    )
    mean = total_sum / channels
    var = total_sq / channels - mean * mean
    normed = (
        (values - mean) * lax.rsqrt(var + 1e-05) * gain_own[:, None, None]
        + shift_own[:, None, None]
    ).astype(jnp.bfloat16)
    along_w = (
        mult("chw,wk->chk", normed, fwd_w).astype(jnp.bfloat16).reshape(local_ch, rows, 2, half)
    )
    first_p = mult("kh,chpq->ckpq", cos_h, along_w)
    first_q = mult("kh,chpq->ckpq", sin_h, along_w)
    modes = jnp.stack(
        [
            (first_p[:, :, 0] + first_q[:, :, 1]).astype(jnp.bfloat16),
            (first_p[:, :, 1] - first_q[:, :, 0]).astype(jnp.bfloat16),
        ],
        axis=2,
    )
    spread = lax.all_to_all(modes, "grid", split_axis=1, concat_axis=0, tiled=True)
    shr_re, shr_im = mix_modes(
        spread[:, :, 0], spread[:, :, 1], first_weight, second_weight, first_bias
    )
    gathered = lax.all_to_all(
        jnp.stack([shr_re, shr_im], axis=2), "grid", split_axis=0, concat_axis=1, tiled=True
    )
    back_p = mult("kh,ckpq->chpq", cos_h, gathered)
    back_q = mult("kh,ckpq->chpq", sin_h, gathered)
    back_re = (back_p[:, :, 0] - back_q[:, :, 1]).astype(jnp.bfloat16)
    back_im = (back_p[:, :, 1] + back_q[:, :, 0]).astype(jnp.bfloat16)
    backed = jnp.concatenate([back_re, back_im], axis=2)
    filtered = mult("chk,kw->chw", backed, inv_w)
    return (values + filtered).astype(jnp.bfloat16)


def solution(mesh):
    return jax.shard_map(
        per_device,
        mesh=mesh,
        in_specs=(P(("batch", "grid"), None, None), P(), P(), P(), P(), P()),
        out_specs=P(("batch", "grid"), None, None),
        check_vma=False,
    )
```

profile of v0, /device:TPU:0, one launch (start us, length us, event | category | flops | bytes accessed | tf_op | source)
XLA Modules:
  0.0 897.6 jit_solution(17641309086073437033)
XLA Ops:
  6.5 0.0 all-reduce.3.cloned.1.call-start
  6.5 8.9 convert_reduce_fusion
  15.4 0.0 all-reduce.3.cloned.1.call-update
  15.4 0.0 copy-done.5
  15.4 0.1 dynamic_slice.6
  15.5 0.0 copy-done.6
  15.5 0.1 dynamic_slice.7
  15.6 2.2 multiply_convert_fusion.6
  17.8 62.3 %all-reduce.3.cloned.1.call-done = (f32[512,512]{1,0:T(8,128)}, f32[512,512]{1,0:T(8,128)}) async-done(((f32[512,512]{1,0:T(8,128)}, f32[512,512]{1,0:T(8,128)}), (f32[512,512]{1,0:T(8,128)}, f32[512,512]{1,0:T(8,128)})) %all-reduce.3.cloned.1.call-update) | async-done | bytes 2097168 | tf_op jit(solution)/shard_map/psum | solution.py:85
  80.2 1.8 broadcast_multiply_fusion
  82.0 16.8 %fusion.28 = bf16[32,512,512]{1,2,0:T(8,128)(2,1)} fusion(bf16[32,512,512]{2,1,0:T(8,128)(2,1)} %param.6, f32[32]{0:T(128)S(1)} %dynamic_slice.7, f32[32]{0:T(128)S(1)} %dynamic_slice.6, f32[512,512]{1,0:T(8,128)S(1)} %get-tuple-element.16, f32[512,512]{1,0:T(8,128)S(1)} %get-tuple-element.15, bf16[512,256]{0,1:T(8,128)(2,1)S(1)} %get-tuple-element.19, ...), kind=kOutput, calls=%fused_computation.48 | convolution fusion | flops 8649703424 | bytes 36176128 | tf_op jit(solution)/shard_map/chw,wk->chk/dot_general | solution.py:39
  98.8 24.6 %convolution_bitcast_fusion.2 = f32[32,512,2,256]{1,3,2,0:T(8,128)} fusion(bf16[32,512,2,256]{1,3,2,0:T(8,128)(2,1)} %bitcast.117), kind=kOutput, calls=%fused_computation.46 | convolution fusion | flops 8594128896 | bytes 50331648 | tf_op jit(solution)/shard_map/kh,chpq->ckpq/dot_general | solution.py:39
  123.4 24.6 %convolution_bitcast_fusion.3 = f32[32,512,2,256]{1,3,2,0:T(8,128)} fusion(bf16[32,512,2,256]{1,3,2,0:T(8,128)(2,1)} %bitcast.118), kind=kOutput, calls=%fused_computation.47 | convolution fusion | flops 8594128896 | bytes 50331648 | tf_op jit(solution)/shard_map/kh,chpq->ckpq/dot_general | solution.py:39
  148.0 25.6 %fusion.18 = (bf16[32,512,1,256]{1,3,2,0:T(8,128)(2,1)S(1)}, bf16[32,512,1,256]{1,3,2,0:T(8,128)(2,1)}) fusion(f32[32,512,2,256]{1,3,2,0:T(8,128)} %convolution_bitcast_fusion.2, f32[32,512,2,256]{1,3,2,0:T(8,128)} %convolution_bitcast_fusion.3), kind=kLoop, calls=%fused_computation.31 | loop fusion | flops 16777216 | bytes 83886080 | tf_op jit(solution)/shard_map/convert_element_type | solution.py:101
  173.6 10.5 %pad_maximum_fusion = bf16[32,512,2,256]{1,3,2,0:T(8,128)(2,1)} fusion(bf16[32,512,1,256]{1,3,2,0:T(8,128)(2,1)} %get-tuple-element.12, bf16[32,512,1,256]{1,3,2,0:T(8,128)(2,1)S(1)} %get-tuple-element.11), kind=kLoop, calls=%fused_computation.32 | loop fusion | flops 8388608 | bytes 33554432 | tf_op jit(solution)/shard_map/stack | solution.py:99
  184.1 41.4 %copy.43 = bf16[32,512,2,256]{3,2,0,1:T(2,128)(2,1)} copy(bf16[32,512,2,256]{1,3,2,0:T(8,128)(2,1)} %pad_maximum_fusion) | data formatting | bytes 33554432 | tf_op jit(solution)/shard_map/stack | solution.py:99
  225.4 5.9 all-to-all-start
  231.3 0.0 copy-done.4
  231.3 0.1 add.121
  231.4 0.1 add.125
  231.5 183.7 %all-to-all-done = bf16[32,512,2,256]{3,2,0,1:T(2,128)(2,1)} async-done(((bf16[32,512,2,256]{3,2,0,1:T(2,128)(2,1)}), bf16[32,512,2,256]{3,2,0,1:T(2,128)(2,1)}, u32[]{:S(2)}, u32[]{:S(2)}) %all-to-all-start) | async-done | bytes 16777248 | tf_op jit(solution)/shard_map/all_to_all | solution.py:106
  415.2 10.4 %copy.44 = bf16[32,512,2,256]{3,1,2,0:T(8,128)(2,1)S(1)} copy(bf16[32,512,2,256]{3,2,0,1:T(2,128)(2,1)} %all-to-all-done) | data formatting | bytes 33554432 | tf_op jit(solution)/shard_map/all_to_all | solution.py:106
  425.7 2.3 copy.45
  428.0 6.4 fusion.104
  434.4 13.5 %reshape_squeeze.6 = bf16[8,32,16384]{2,1,0:T(8,128)(2,1)} reshape(bf16[256,64,1,256]{3,1,2,0:T(8,128)(2,1)} %get-tuple-element.13) | data formatting | bytes 16777216 | tf_op jit(solution)/shard_map/reshape;squeeze | solution.py:50
  447.9 13.5 %reshape_squeeze.7 = bf16[8,32,16384]{2,1,0:T(8,128)(2,1)} reshape(bf16[256,64,1,256]{3,1,2,0:T(8,128)(2,1)} %get-tuple-element.14) | data formatting | bytes 16777216 | tf_op jit(solution)/shard_map/reshape;squeeze | solution.py:51
  461.4 11.6 %fusion.72 = f32[8,16384,32]{1,2,0:T(8,128)} fusion(bf16[8,32,16384]{2,1,0:T(8,128)(2,1)} %reshape_squeeze.6, bf16[2,8,32,32]{3,2,1,0:T(8,128)(2,1)S(1)} %copy-done.3), kind=kOutput, calls=%fused_computation.105 | convolution fusion | flops 268435456 | bytes 25231360 | tf_op jit(solution)/shard_map/bio,bim->bom/dot_general | solution.py:39
  473.0 0.0 copy-done.1
  473.0 7.6 fusion.70
  480.7 0.0 copy-start.2
  480.7 13.9 %fusion.11 = bf16[8,16384,32]{1,2,0:T(8,128)(2,1)} fusion(f32[8,16384,32]{1,2,0:T(8,128)} %fusion.72, bf16[8,32,16384]{2,1,0:T(8,128)(2,1)} %reshape_squeeze.7, f32[8,32]{1,0:T(8,128)S(1)} %add.121, bf16[2,8,32,32]{3,2,1,0:T(8,128)(2,1)S(1)} %copy-done.3), kind=kOutput, calls=%fused_computation.19 | convolution fusion | flops 285212672 | bytes 33624064 | tf_op jit(solution)/shard_map/bio,bim->bom/dot_general | solution.py:39
  494.6 11.5 %fusion.66 = f32[8,16384,32]{1,2,0:T(8,128)} fusion(bf16[8,16384,32]{1,2,0:T(8,128)(2,1)} %fusion.11, bf16[2,8,32,32]{3,2,1,0:T(8,128)(2,1)S(1)} %copy-done.2), kind=kOutput, calls=%fused_computation.99 | convolution fusion | flops 268435456 | bytes 25231360 | tf_op jit(solution)/shard_map/bio,bim->bom/dot_general | solution.py:39
  506.1 13.9 %fusion.10 = bf16[8,16384,32]{1,2,0:T(8,128)(2,1)} fusion(f32[8,16384,32]{1,2,0:T(8,128)} %fusion.70, bf16[8,32,16384]{2,1,0:T(8,128)(2,1)} %reshape_squeeze.6, f32[8,32]{1,0:T(8,128)S(1)} %add.125, bf16[2,8,32,32]{3,2,1,0:T(8,128)(2,1)S(1)} %copy-done.3), kind=kOutput, calls=%fused_computation.18 | convolution fusion | flops 285212672 | bytes 33624064 | tf_op jit(solution)/shard_map/bio,bim->bom/dot_general | solution.py:39
  520.0 12.1 %fusion.64 = f32[8,16384,32]{1,2,0:T(8,128)} fusion(bf16[8,16384,32]{1,2,0:T(8,128)(2,1)} %fusion.10, bf16[2,8,32,32]{3,2,1,0:T(8,128)(2,1)S(1)} %copy-done.2), kind=kOutput, calls=%fused_computation.97 | convolution fusion | flops 268435456 | bytes 25231360 | tf_op jit(solution)/shard_map/bio,bim->bom/dot_general | solution.py:39
  532.0 10.3 %add_convert_fusion.1 = bf16[8,16384,32]{1,2,0:T(8,128)(2,1)} fusion(f32[8,16384,32]{1,2,0:T(8,128)} %fusion.66, bf16[8,16384,32]{1,2,0:T(8,128)(2,1)S(1)} %copy-done, bf16[2,8,32,32]{3,2,1,0:T(8,128)(2,1)S(1)} %copy-done.2), kind=kOutput, calls=%fused_computation.40 | convolution fusion | flops 297795584 | bytes 33619968 | tf_op jit(solution)/shard_map/bio,bim->bom/dot_general | solution.py:39
  542.3 9.4 %copy.71 = bf16[32,8,64,256]{3,2,1,0:T(8,128)(2,1)} copy(bf16[32,8,64,256]{3,1,2,0:T(8,128)(2,1)} %bitcast.123) | data formatting | bytes 16777216
  551.7 13.2 %add_convert_fusion = bf16[8,16384,32]{1,2,0:T(8,128)(2,1)} fusion(f32[8,16384,32]{1,2,0:T(8,128)} %fusion.64, bf16[8,16384,32]{1,2,0:T(8,128)(2,1)} %fusion.11, bf16[2,8,32,32]{3,2,1,0:T(8,128)(2,1)S(1)} %copy-done.2), kind=kOutput, calls=%fused_computation.39 | convolution fusion | flops 297795584 | bytes 33619968 | tf_op jit(solution)/shard_map/bio,bim->bom/dot_general | solution.py:39
  564.9 9.4 %copy.72 = bf16[32,8,64,256]{3,2,1,0:T(8,128)(2,1)} copy(bf16[32,8,64,256]{3,1,2,0:T(8,128)(2,1)} %bitcast.124) | data formatting | bytes 16777216
  574.3 13.8 %pad_maximum_fusion.1 = bf16[256,64,2,256]{3,1,2,0:T(8,128)(2,1)} fusion(bf16[256,64,1,256]{3,1,2,0:T(8,128)(2,1)} %bitcast.126, bf16[256,64,1,256]{3,1,2,0:T(8,128)(2,1)} %bitcast.125), kind=kLoop, calls=%fused_computation.33 | loop fusion | flops 8388608 | bytes 33554432 | tf_op jit(solution)/shard_map/stack | solution.py:111
  588.2 5.9 all-to-all-start.1
  594.1 2.3 multiply_convert_fusion.3
  596.4 181.6 %all-to-all-done.1 = bf16[256,64,2,256]{3,1,2,0:T(8,128)(2,1)} async-done(((bf16[256,64,2,256]{3,1,2,0:T(8,128)(2,1)}), bf16[256,64,2,256]{3,1,2,0:T(8,128)(2,1)}, u32[]{:S(2)}, u32[]{:S(2)}) %all-to-all-start.1) | async-done | bytes 16777248 | tf_op jit(solution)/shard_map/all_to_all | solution.py:110
  778.0 14.2 %copy.52 = bf16[32,8,64,2,256]{4,2,1,3,0:T(8,128)(2,1)} copy(bf16[32,8,64,2,256]{4,2,3,0,1:T(8,128)(2,1)} %bitcast.20) | data formatting | bytes 33554432 | tf_op jit(solution)/shard_map/all_to_all | solution.py:110
  792.2 22.1 %convolution_bitcast_fusion = f32[32,512,2,256]{1,3,0,2:T(8,128)} fusion(bf16[32,512,2,256]{3,1,2,0:T(8,128)(2,1)} %bitcast.119), kind=kOutput, calls=%fused_computation.20 | convolution fusion | flops 8594128896 | bytes 50331648 | tf_op jit(solution)/shard_map/kh,ckpq->chpq/dot_general | solution.py:39
  814.3 24.7 %convolution_bitcast_fusion.1 = f32[32,512,2,256]{1,3,2,0:T(8,128)} fusion(bf16[32,512,2,256]{3,1,2,0:T(8,128)(2,1)} %bitcast.120), kind=kOutput, calls=%fused_computation.45 | convolution fusion | flops 8594128896 | bytes 50331648 | tf_op jit(solution)/shard_map/kh,ckpq->chpq/dot_general | solution.py:39
  839.0 15.1 %fusion.33 = bf16[32,512,256]{1,2,0:T(8,128)(2,1)} fusion(f32[32,512,2,256]{1,3,0,2:T(8,128)} %convolution_bitcast_fusion, f32[32,512,2,256]{1,3,2,0:T(8,128)} %convolution_bitcast_fusion.1), kind=kLoop, calls=%fused_computation.49 | loop fusion | flops 8388608 | bytes 41943040 | tf_op jit(solution)/shard_map/convert_element_type | solution.py:115
  854.1 15.1 %fusion.34 = bf16[32,512,256]{1,2,0:T(8,128)(2,1)} fusion(f32[32,512,2,256]{1,3,0,2:T(8,128)} %convolution_bitcast_fusion, f32[32,512,2,256]{1,3,2,0:T(8,128)} %convolution_bitcast_fusion.1), kind=kLoop, calls=%fused_computation.50 | loop fusion | flops 8388608 | bytes 41943040 | tf_op jit(solution)/shard_map/convert_element_type | solution.py:116
  869.2 21.3 %fusion.5 = bf16[32,512,512]{2,1,0:T(8,128)(2,1)} fusion(bf16[32,512,512]{2,1,0:T(8,128)(2,1)} %param.6, bf16[32,512,256]{1,2,0:T(8,128)(2,1)} %fusion.34, bf16[32,512,256]{1,2,0:T(8,128)(2,1)} %fusion.33, bf16[256,512]{1,0:T(8,128)(2,1)S(1)} %get-tuple-element.18, bf16[256,512]{1,0:T(8,128)(2,1)S(1)} %get-tuple-element.17), kind=kOutput, calls=%fused_computation.9 | convolution fusion | flops 8649703424 | bytes 50855936 | tf_op jit(solution)/shard_map/chk,kw->chw/dot_general | solution.py:39
  (11 shorter events, 0.0 us)
Async XLA Ops:
  6.5 8.9 copy-start.5
  6.5 9.0 %copy-start.6 = (f32[256]{0:T(256)S(1)}, f32[256]{0:T(256)}, u32[]{:S(2)}) copy-start(f32[256]{0:T(256)} %param.8) | copy-start | bytes 3076
  6.5 73.6 %all-reduce.3.cloned.1.call-start = ((), (), s32[]{:S(2)}) async-start(), calls=%async_computation.2 | async-start | bytes 4194304 | tf_op jit(solution)/shard_map/psum | solution.py:85
  225.4 5.9 copy-start.4
  225.4 189.8 %all-to-all-start = ((bf16[32,512,2,256]{3,2,0,1:T(2,128)(2,1)}), bf16[32,512,2,256]{3,2,0,1:T(2,128)(2,1)}, u32[]{:S(2)}, u32[]{:S(2)}) async-start(bf16[32,512,2,256]{3,2,0,1:T(2,128)(2,1)} %copy.43), calls=%async_computation | async-start | bytes 33554432 | tf_op jit(solution)/shard_map/all_to_all | solution.py:106
  434.4 27.0 %copy-start.3 = (bf16[2,8,32,32]{3,2,1,0:T(8,128)(2,1)S(1)}, bf16[2,8,32,32]{3,2,1,0:T(8,128)(2,1)}, u32[]{:S(2)}) copy-start(bf16[2,8,32,32]{3,2,1,0:T(8,128)(2,1)} %param.9) | copy-start | bytes 98308
  461.4 11.6 %copy-start.1 = (bf16[8,32,16384]{2,1,0:T(8,128)(2,1)S(1)}, bf16[8,32,16384]{2,1,0:T(8,128)(2,1)}, u32[]{:S(2)}) copy-start(bf16[8,32,16384]{2,1,0:T(8,128)(2,1)} %reshape_squeeze.7) | copy-start | bytes 25165828
  480.7 13.9 %copy-start.2 = (bf16[2,8,32,32]{3,2,1,0:T(8,128)(2,1)S(1)}, bf16[2,8,32,32]{3,2,1,0:T(8,128)(2,1)}, u32[]{:S(2)}) copy-start(bf16[2,8,32,32]{3,2,1,0:T(8,128)(2,1)} %param.10) | copy-start | bytes 98308
  520.0 12.1 %copy-start = (bf16[8,16384,32]{1,2,0:T(8,128)(2,1)S(1)}, bf16[8,16384,32]{1,2,0:T(8,128)(2,1)}, u32[]{:S(2)}) copy-start(bf16[8,16384,32]{1,2,0:T(8,128)(2,1)} %fusion.10) | copy-start | bytes 25165828
  588.2 189.9 %all-to-all-start.1 = ((bf16[256,64,2,256]{3,1,2,0:T(8,128)(2,1)}), bf16[256,64,2,256]{3,1,2,0:T(8,128)(2,1)}, u32[]{:S(2)}, u32[]{:S(2)}) async-start(bf16[256,64,2,256]{3,1,2,0:T(8,128)(2,1)} %pad_maximum_fusion.1), calls=%async_computation.1 | async-start | bytes 33554432 | tf_op jit(solution)/shard_map/all_to_all | solution.py:110
Sparse Core Ops, SparseCore 0:
  15.6 64.5 all-reduce.2
where the time goes:
time: 909 us; the launch traced here: 898 us
  waiting for transfers between devices  428 us (47%)
  matrix products  228 us (25%)
  local copies, waits for them, and re-layouts  121 us (13%)
  other arithmetic  95.3 us (10%)
  between operations  13.7 us (2%)
  starting transfers between devices  11.8 us (1%)
    dot_general x14, matrix products, mult(): return jnp.einsum(form, left, right, preferred_element_type=jnp.float32)  228 us
    all_to_all x1, waiting for transfers between devices, per_device(): lax.all_to_all(modes, 'grid', split_axis=1, concat_axis=0, tiled=True)  184 us
    all_to_all x1, waiting for transfers between devices, per_device(): lax.all_to_all(jnp.stack([shr_re, shr_im], axis=2), 'grid', split_axis=0,...  182 us
    psum x1, waiting for transfers between devices, per_device(): lax.psum((jnp.sum(values, axis=0), jnp.sum(values * values, axis=0)), 'gr...  62.3 us
    another operation x1, local copies, waits for them, and re-layouts, per_device(): jnp.stack([(first_p[:, :, 0] + first_q[:, :, 1]).astype(jnp.bfloat16), (f...  41.4 us
    convert_element_type x1, other arithmetic, per_device(): (first_p[:, :, 0] + first_q[:, :, 1]).astype(jnp.bfloat16)  25.6 us
    unnamed x16, local copies, waits for them, and re-layouts  18.8 us
  transfers between devices with their start and end apart: 3, of which 3 were waited for; matrix products, arithmetic and copies ran while one was open for 1% of the time, Pallas kernels for 0%

commit v1 on v0

v1 whole, which is shorter than its diff:
```python
import functools
import math

import jax
import jax.numpy as jnp
from jax import lax
from jax.experimental import pallas as pl
from jax.experimental.pallas import tpu as pltpu
from jax.sharding import PartitionSpec as P

LANES = 128
F32 = jnp.float32
BF16 = jnp.bfloat16


def tables(rows, cols):
    half = cols // 2
    col_index = jnp.arange(cols, dtype=jnp.int32)
    mode_index = jnp.arange(half, dtype=jnp.int32)
    angle_w = (col_index[:, None] * mode_index[None, :] % cols).astype(F32) * (
        2.0 * math.pi / cols
    )
    scale_w = 1.0 / math.sqrt(cols)
    fwd_w = jnp.concatenate(
        [jnp.cos(angle_w) * scale_w, -jnp.sin(angle_w) * scale_w], axis=1
    ).astype(BF16)
    weight_k = jnp.where(mode_index == 0, 1.0, 2.0).astype(F32)
    inv_w = jnp.concatenate(
        [
            (jnp.cos(angle_w) * weight_k[None, :] * scale_w).T,
            (-jnp.sin(angle_w) * weight_k[None, :] * scale_w).T,
        ],
        axis=0,
    ).astype(BF16)
    mid = rows // 2
    row_index = jnp.arange(rows, dtype=jnp.int32)
    k_index = jnp.arange(mid, dtype=jnp.int32)
    angle_h = (k_index[:, None] * row_index[None, :] % rows).astype(F32) * (2.0 * math.pi / rows)
    scale_h = 1.0 / math.sqrt(rows)
    nyquist = jnp.where(row_index % 2 == 0, scale_h, -scale_h).astype(F32)
    cos_h = jnp.cos(angle_h) * scale_h
    sin_h = jnp.where(k_index[:, None] == 0, nyquist[None, :], jnp.sin(angle_h) * scale_h)
    half_h = jnp.concatenate([cos_h, sin_h], axis=0).astype(BF16)
    return fwd_w, inv_w, half_h, half_h.T


def forward_kernel(gain, shift, x, mean, rstd, fwd_w, half_h, out):
    c = pl.program_id(0)
    mid = out.shape[2]
    half = out.shape[3] // 2
    values = x[0].astype(F32)
    normed = ((values - mean[...]) * rstd[...] * gain[c] + shift[c]).astype(BF16)
    along = jnp.dot(normed, fwd_w[...], preferred_element_type=F32).astype(BF16)
    both = jnp.dot(half_h[...], along, preferred_element_type=F32)
    c_re, c_im = both[:mid, :half], both[:mid, half:]
    s_re, s_im = both[mid:, :half], both[mid:, half:]
    first = lax.broadcasted_iota(jnp.int32, c_re.shape, 0) == 0
    out[0, 0, :, :half] = jnp.where(first, c_re, c_re + s_im).astype(BF16)
    out[0, 0, :, half:] = jnp.where(first, c_im, c_im - s_re).astype(BF16)
    out[0, 1, :, :half] = jnp.where(first, s_re, c_re - s_im).astype(BF16)
    out[0, 1, :, half:] = jnp.where(first, s_im, c_im + s_re).astype(BF16)


def shrink(values):
    return jnp.maximum(values - 0.01, 0.0) + jnp.minimum(values + 0.01, 0.0)


def mix_kernel(has_zero, x, w1, w2, bias, out, src, dst, *, rep):
    width, _, kt, cols = x.shape
    half = cols // 2
    chunks = cols // LANES
    hc = chunks // 2
    for ab in range(2):
        for l in range(chunks):
            src[ab, l] = (
                x[:, ab, :, l * LANES : (l + 1) * LANES].astype(F32).reshape(width * kt, LANES)
            )
    for ab in range(2):
        for k0 in range(0, kt, rep):
            rows = []
            for k in range(k0, k0 + rep):
                for ri in range(2):
                    rows.append(
                        jnp.concatenate(
                            [
                                src[ab, ri * hc + l, pl.ds(k, width, stride=kt), :]
                                for l in range(hc)
                            ],
                            axis=1,
                        )
                    )
            stack = jnp.concatenate(rows, axis=0).astype(BF16)
            hid = jnp.dot(w1[0], stack, preferred_element_type=F32) + bias[0]
            hid = jnp.maximum(hid, 0.0).astype(BF16)
            res = shrink(jnp.dot(w2[0], hid, preferred_element_type=F32))
            for i in range(rep):
                for ri in range(2):
                    r0 = (i * 2 + ri) * width
                    for l in range(hc):
                        dst[ab, ri * hc + l, pl.ds(k0 + i, width, stride=kt), :] = res[
                            r0 : r0 + width, l * LANES : (l + 1) * LANES
                        ]
    row = lax.broadcasted_iota(jnp.int32, (width, kt, LANES), 1)
    first = (row == 0) & ((pl.program_id(1) == 0) & (has_zero[0] == 1))
    for l in range(hc):
        shape = (width, kt, LANES)
        a_re, b_re = dst[0, l].reshape(shape), dst[1, l].reshape(shape)
        a_im, b_im = dst[0, hc + l].reshape(shape), dst[1, hc + l].reshape(shape)
        lo = slice(l * LANES, (l + 1) * LANES)
        hi = slice(half + l * LANES, half + (l + 1) * LANES)
        out[:, 0, :, lo] = jnp.where(first, a_re, a_re + b_re).astype(BF16)
        out[:, 0, :, hi] = jnp.where(first, a_im, a_im + b_im).astype(BF16)
        out[:, 1, :, lo] = jnp.where(first, b_re, b_im - a_im).astype(BF16)
        out[:, 1, :, hi] = jnp.where(first, b_im, a_re - b_re).astype(BF16)


def inverse_kernel(y, x, half_t, inv_w, out):
    rows, cols = y.shape[1] * y.shape[2], y.shape[3]
    back = jnp.dot(half_t[...], y[0].reshape(rows, cols), preferred_element_type=F32).astype(BF16)
    filtered = jnp.dot(back, inv_w[...], preferred_element_type=F32)
    out[0] = (x[0].astype(F32) + filtered).astype(BF16)


def real_form(weight, rep):
    re = jnp.swapaxes(weight[0], 1, 2)
    im = jnp.swapaxes(weight[1], 1, 2)
    whole = jnp.concatenate(
        [jnp.concatenate([re, -im], axis=2), jnp.concatenate([im, re], axis=2)], axis=1
    )
    n, size, _ = whole.shape
    eye = jnp.eye(rep, dtype=whole.dtype)
    return (eye[None, :, None, :, None] * whole[:, None, :, None, :]).reshape(
        n, rep * size, rep * size
    )


def per_device(fields, norm_gain, norm_shift, first_weight, second_weight, first_bias):
    local_ch, rows, cols = fields.shape
    half, mid = cols // 2, rows // 2
    groups = lax.axis_size("grid")
    channels = local_ch * groups
    width = first_weight.shape[2]
    fwd_w, inv_w, half_h, half_t = tables(rows, cols)
    position = lax.axis_index("grid")
    start = position * local_ch
    gain_own = lax.dynamic_slice_in_dim(norm_gain, start, local_ch)
    shift_own = lax.dynamic_slice_in_dim(norm_shift, start, local_ch)
    values = fields.astype(F32)
    total_sum, total_sq = lax.psum(
        (jnp.sum(values, axis=0), jnp.sum(values * values, axis=0)), "grid"
    )
    mean = total_sum / channels
    rstd = lax.rsqrt(total_sq / channels - mean * mean + 1e-05)

    whole = lambda shape: pl.BlockSpec(shape, lambda *_: (0,) * len(shape))
    one = pl.BlockSpec((1, rows, cols), lambda c: (c, 0, 0))
    one4 = pl.BlockSpec((1, 2, mid, cols), lambda c: (c, 0, 0, 0))
    smem = pl.BlockSpec(memory_space=pltpu.SMEM)
    flops = 4 * local_ch * rows * cols * cols
    modes = pl.pallas_call(
        forward_kernel,
        grid=(local_ch,),
        in_specs=[smem, smem, one, whole((rows, cols)), whole((rows, cols)),
                  whole((cols, cols)), whole((rows, rows))],
        out_specs=one4,
        out_shape=jax.ShapeDtypeStruct((local_ch, 2, mid, cols), BF16),
        cost_estimate=pl.CostEstimate(
            flops=flops, bytes_accessed=4 * fields.size, transcendentals=0
        ),
        name="forward",
    )(gain_own, shift_own, fields, mean, rstd, fwd_w, half_h)

    share = max(1, width // local_ch)
    pieces = [list(range(i, i + share)) for i in range(0, groups, share)]
    if share > 1:
        modes = lax.all_to_all(
            modes, "grid", split_axis=2, concat_axis=0, axis_index_groups=pieces, tiled=True
        )
    own_blocks = modes.shape[0] // width
    first_block = start // width
    own = lambda w, axis: lax.dynamic_slice_in_dim(w, first_block, own_blocks, axis)
    rep = max(1, 256 // (2 * width))
    w1 = real_form(own(first_weight, 1), rep)
    w2 = real_form(own(second_weight, 1), rep)
    bias = jnp.swapaxes(own(first_bias.reshape(2, -1, width), 1), 0, 1).reshape(own_blocks, -1)
    bias = jnp.tile(bias, (1, rep))[:, :, None]
    has_zero = (position % share == 0).astype(jnp.int32).reshape(1)
    own_k = modes.shape[2]
    kt = min(16, own_k)
    size = rep * 2 * width
    tile = pl.BlockSpec((width, 2, kt, cols), lambda b, k: (b, 0, k, 0))
    per_block = lambda n: pl.BlockSpec((1, size, n), lambda b, k: (b, 0, 0))
    scratch = pltpu.VMEM((2, cols // LANES, width * kt, LANES), F32)
    mixed = pl.pallas_call(
        functools.partial(mix_kernel, rep=rep),
        grid=(own_blocks, own_k // kt),
        in_specs=[smem, tile, per_block(size), per_block(size), per_block(1)],
        out_specs=tile,
        out_shape=jax.ShapeDtypeStruct(modes.shape, BF16),
        scratch_shapes=[scratch, scratch],
        cost_estimate=pl.CostEstimate(
            flops=16 * width * modes.size, bytes_accessed=4 * modes.size, transcendentals=0
        ),
        name="mix",
    )(has_zero, modes, w1, w2, bias)
    if share > 1:
        mixed = lax.all_to_all(
            mixed, "grid", split_axis=0, concat_axis=2, axis_index_groups=pieces, tiled=True
        )
    return pl.pallas_call(
        inverse_kernel,
        grid=(local_ch,),
        in_specs=[one4, one, whole((rows, rows)), whole((cols, cols))],
        out_specs=one,
        out_shape=jax.ShapeDtypeStruct(fields.shape, BF16),
        cost_estimate=pl.CostEstimate(
            flops=flops, bytes_accessed=6 * fields.size, transcendentals=0
        ),
        name="inverse",
    )(mixed, fields, half_t, inv_w)


def solution(mesh):
    return jax.shard_map(
        per_device,
        mesh=mesh,
        in_specs=(P(("batch", "grid"), None, None), P(), P(), P(), P(), P()),
        out_specs=P(("batch", "grid"), None, None),
        check_vma=False,
    )
```

time: 909 us -> 206 us (0.23); the launches traced: 898 us -> 204 us
  waiting for transfers between devices: 428 us -> 46.6 us
  matrix products: 228 us -> 0 us
  local copies, waits for them, and re-layouts: 121 us -> 5.88 us
  Pallas kernels: 0 us -> 114 us
  other arithmetic: 95.3 us -> 24.3 us
  starting transfers between devices: 11.8 us -> 0.01 us
    all_to_all x2 -> x0, waiting for transfers between devices: 365 us -> none  [the longest x1 184 us: per_device(): lax.all_to_all(modes, 'grid', split_axis=1, concat_axis=0, tiled=True)]
    dot_general x14 -> x0, matrix products: 228 us -> none  [mult(): return jnp.einsum(form, left, right, preferred_element_type=jnp.float32)]
    pallas_call x0 -> x3, Pallas kernels: none -> 114 us  [the longest x1 41.5 us: per_device(): pl.pallas_call(functools.partial(mix_kernel, rep=rep), grid=(own_blocks,...]
    another operation x3, local copies, waits for them, and re-layouts: 68.3 us -> 0.89 us  [per_device(): bias = jnp.tile(bias, (1, rep))[:, :, None]]
    convert_element_type x3 -> x1, other arithmetic: 55.7 us -> 0.01 us  [real_form(): eye = jnp.eye(rep, dtype=whole.dtype)]
    all_to_all x3 -> x0, local copies, waits for them, and re-layouts: 26.9 us -> none  [the longest x1 14.2 us: per_device(): lax.all_to_all(jnp.stack([shr_re, shr_im], axis=2), 'grid', split_axis=0,...]
    another operation x4, other arithmetic: 28.8 us -> 8.5 us  [the longest x1 13.8 us: per_device(): jnp.stack([shr_re, shr_im], axis=2)]
    unnamed x16 -> x6, local copies, waits for them, and re-layouts: 18.8 us -> 0.01 us
  transfers between devices with their start and end apart: 3 -> 1, of which waited for: 3 -> 1; matrix products, arithmetic and copies ran while one was open for 1% -> 9% of each run, Pallas kernels for 0% -> 0%
where the time goes in v1:
time: 206 us; the launch traced here: 204 us
  Pallas kernels  114 us (55%)
  waiting for transfers between devices  46.6 us (23%)
  other arithmetic  24.3 us (12%)
  between operations  13.5 us (7%)
  local copies, waits for them, and re-layouts  5.88 us (3%)
    psum x1, waiting for transfers between devices, per_device(): lax.psum((jnp.sum(values, axis=0), jnp.sum(values * values, axis=0)), 'gr...  46.6 us
    pallas_call x1, Pallas kernels, per_device(): pl.pallas_call(functools.partial(mix_kernel, rep=rep), grid=(own_blocks,...  41.5 us
    pallas_call x1, Pallas kernels, per_device(): pl.pallas_call(inverse_kernel, grid=(local_ch,), in_specs=[one4, one, who...  36.7 us
    pallas_call x1, Pallas kernels, per_device(): pl.pallas_call(forward_kernel, grid=(local_ch,), in_specs=[smem, smem, on...  35.9 us
    reduce_sum x1, other arithmetic, per_device(): jnp.sum(values * values, axis=0)  8.87 us
    another operation x4, other arithmetic  8.5 us
  transfers between devices with their start and end apart: 1, of which 1 were waited for; matrix products, arithmetic and copies ran while one was open for 9% of the time, Pallas kernels for 0%

profile of v1, /device:TPU:0, one launch (start us, length us, event | category | flops | bytes accessed | tf_op | source)
XLA Modules:
  0.0 204.3 jit_solution(12519157160154359233)
XLA Ops:
  6.5 0.0 copy-start
  6.5 0.0 copy-start.1
  6.5 0.0 copy-start.2
  6.5 0.0 all-reduce.3.cloned.1.call-start
  6.5 8.9 %fusion = (f32[512,512]{1,0:T(8,128)}, f32[512,512]{1,0:T(8,128)}) fusion(bf16[32,512,512]{2,1,0:T(8,128)(2,1)} %x.3), kind=kLoop, calls=%fused_computation.2 | loop fusion | flops 33030144 | bytes 18874368 | tf_op jit(solution)/shard_map/reduce_sum | solution.py:150
  15.4 0.0 all-reduce.3.cloned.1.call-update
  15.5 2.0 multiply_convert_fusion.2
  17.5 0.7 dynamic-slice_bitcast_fusion.1
  18.2 0.7 fusion.22
  18.9 0.1 maximum_bitcast_fusion
  19.0 0.1 copy.11
  19.1 0.1 maximum_bitcast_fusion.1
  19.2 0.1 copy.12
  19.3 0.3 broadcast_multiply_fusion.1
  19.6 0.9 mul.196.w1
  20.4 0.9 mul.200.w2
  21.3 0.0 copy-done
  21.3 0.1 reshape.95
  21.4 0.1 tile.9
  21.5 0.8 tile.12.bias
  22.3 0.0 copy-done.1
  22.3 0.6 dynamic_slice.15.gain
  22.9 0.0 copy-done.2
  22.9 0.7 dynamic_slice.16.shift
  23.6 2.1 %select_convert_fusion = bf16[256,512]{1,0:T(8,128)(2,1)S(1)} fusion(bf16[512]{0:T(512)(128)(2,1)S(1)} %fusion.18, pred[256]{0:T(512)(128)(4,1)S(1)} %iota_compare_fusion.1), kind=kLoop, calls=%fused_computation.21 | loop fusion | flops 2097152 | bytes 263424 | tf_op jit(solution)/shard_map/convert.3
  25.6 0.9 fusion.21
  26.5 1.0 copy.15.half_t
  27.5 2.2 %multiply_convert_fusion.3 = (bf16[512,256]{1,0:T(8,128)(2,1)S(1)}, bf16[512,256]{1,0:T(8,128)(2,1)S(1)}) fusion(), kind=kLoop, calls=%fused_computation.25 | loop fusion | flops 2490368 | bytes 524288 | tf_op jit(solution)/shard_map/convert.5
  29.7 0.8 pad_maximum_fusion.fwd_w
  30.5 2.3 %multiply_convert_fusion.1 = (bf16[256,512]{1,0:T(8,128)(2,1)S(1)}, bf16[256,512]{1,0:T(8,128)(2,1)S(1)}) fusion(f32[256]{0:T(256)S(1)} %broadcast_select_fusion), kind=kLoop, calls=%fused_computation.20 | loop fusion | flops 2752512 | bytes 525312 | tf_op jit(solution)/shard_map/convert
  32.8 0.8 pad_maximum_fusion.2.inv_w
  33.6 46.6 %all-reduce.3.cloned.1.call-done = (f32[512,512]{1,0:T(8,128)}, f32[512,512]{1,0:T(8,128)}) async-done(((f32[512,512]{1,0:T(8,128)}, f32[512,512]{1,0:T(8,128)}), (f32[512,512]{1,0:T(8,128)}, f32[512,512]{1,0:T(8,128)})) %all-reduce.3.cloned.1.call-update) | async-done | bytes 2097168 | tf_op jit(solution)/shard_map/psum | solution.py:149
  80.2 3.2 %add_rsqrt_fusion = (f32[512,512]{1,0:T(8,128)}, f32[512,512]{1,0:T(8,128)}) fusion(f32[512,512]{1,0:T(8,128)} %get-tuple-element.8, f32[512,512]{1,0:T(8,128)} %get-tuple-element.7), kind=kLoop, calls=%fused_computation.3 | loop fusion | flops 1310720 | bytes 4194304 | tf_op jit(solution)/shard_map/rsqrt | solution.py:153
  83.4 35.9 %forward.1.x = bf16[32,2,256,512]{3,2,1,0:T(8,128)(2,1)} custom-call(f32[32]{0:T(128)} %dynamic_slice.15.gain, f32[32]{0:T(128)} %dynamic_slice.16.shift, bf16[32,512,512]{2,1,0:T(8,128)(2,1)} %x.3, f32[512,512]{1,0:T(8,128)} %get-tuple-element.14.mean, f32[512,512]{1,0:T(8,128)} %get-tuple-element.13.rstd, bf16[512,512]{1,0:T(8,128)(2,1)} %pad_maximum_fusion.fwd_w, ...), custom_call_target="tpu_custom_call" | custom-call | flops 17179869184 | bytes 33554432 | tf_op jit(solution)/shard_map/forward/pallas_call | solution.py:160
  119.3 41.5 %mix.1.y = bf16[32,2,256,512]{3,2,1,0:T(8,128)(2,1)} custom-call(s32[1]{0:T(128)} %constant.80.clone.1.has_zero, bf16[32,2,256,512]{3,2,1,0:T(8,128)(2,1)} %forward.1.x, bf16[1,256,256]{2,1,0:T(8,128)(2,1)} %mul.196.w1, bf16[1,256,256]{2,1,0:T(8,128)(2,1)} %mul.200.w2, f32[1,256,1]{2,1,0:T(8,128)} %tile.12.bias), custom_call_target="tpu_custom_call" | custom-call | flops 4294967296 | bytes 33554432 | tf_op jit(solution)/shard_map/mix/pallas_call | solution.py:194
  160.8 36.7 %inverse.1 = bf16[32,512,512]{2,1,0:T(8,128)(2,1)} custom-call(bf16[32,2,256,512]{3,2,1,0:T(8,128)(2,1)} %mix.1.y, bf16[32,512,512]{2,1,0:T(8,128)(2,1)} %x.3, bf16[512,512]{1,0:T(8,128)(2,1)} %copy.15.half_t, bf16[512,512]{1,0:T(8,128)(2,1)} %pad_maximum_fusion.2.inv_w), custom_call_target="tpu_custom_call" | custom-call | flops 17179869184 | bytes 50331648 | tf_op jit(solution)/shard_map/inverse/pallas_call | solution.py:210
  (6 shorter events, 0.0 us)
Async XLA Ops:
  6.5 14.8 %copy-start = (f32[2,256]{1,0:T(2,128)S(1)}, f32[2,256]{1,0:T(2,128)}, u32[]{:S(2)}) copy-start(f32[2,256]{1,0:T(2,128)} %param.11) | copy-start | bytes 6148
  6.5 15.8 %copy-start.1 = (f32[256]{0:T(256)S(1)}, f32[256]{0:T(256)}, u32[]{:S(2)}) copy-start(f32[256]{0:T(256)} %param.7) | copy-start | bytes 3076
  6.5 16.3 %copy-start.2 = (f32[256]{0:T(256)S(1)}, f32[256]{0:T(256)}, u32[]{:S(2)}) copy-start(f32[256]{0:T(256)} %param.8) | copy-start | bytes 3076
  6.5 73.7 %all-reduce.3.cloned.1.call-start = ((), (), s32[]{:S(2)}) async-start(), calls=%async_computation | async-start | bytes 4194304 | tf_op jit(solution)/shard_map/psum | solution.py:149
Sparse Core Ops, SparseCore 0:
  15.6 64.6 all-reduce.2
